TPU v7x, 16 devices: a 4x2x1 block of a 4x4x8 slice. The times are simulated.
16 devices in a mesh: rep: 4 (over y, z, core), dp: 4 (over x).
Axes of the slice: x: 4, y: 2, z: 1, core: 2. Of those that a mesh axis runs over, the one named last changes fastest.
The devices are a block of a 4x4x8 slice.
Arguments:
- x: bfloat16 [16, 1024, 1024], P(('rep', 'dp')), parts along dimension 0
- dy: bfloat16 [16, 1024, 1024], P(('rep', 'dp')), parts along dimension 0
- w_gate: bfloat16 [2, 1024, 3200], replicated
- w_up: bfloat16 [2, 1024, 3200], replicated
- w_down: bfloat16 [2, 3200, 1024], replicated
- m_w_gate: float32 [2, 1024, 3200], replicated
- m_w_up: float32 [2, 1024, 3200], replicated
- m_w_down: float32 [2, 3200, 1024], replicated
- v_w_gate: float32 [2, 1024, 3200], replicated
- v_w_up: float32 [2, 1024, 3200], replicated
- v_w_down: float32 [2, 3200, 1024], replicated
Outputs:
- output 1: bfloat16 [8, 1024, 3200], P('rep'), parts along dimension 0
- output 2: bfloat16 [8, 1024, 3200], P('rep'), parts along dimension 0
- output 3: bfloat16 [8, 3200, 1024], P('rep'), parts along dimension 0
- output 4: float32 [8, 1024, 3200], P('rep'), parts along dimension 0
- output 5: float32 [8, 1024, 3200], P('rep'), parts along dimension 0
- output 6: float32 [8, 3200, 1024], P('rep'), parts along dimension 0
- output 7: float32 [8, 1024, 3200], P('rep'), parts along dimension 0
- output 8: float32 [8, 1024, 3200], P('rep'), parts along dimension 0
- output 9: float32 [8, 3200, 1024], P('rep'), parts along dimension 0
There are 4 independent parts. A program takes and returns all parts, laid end to end along the dimension named above; an argument that names none is the same for every part.
All inputs are finite; a program needn't handle non-finite values.
Results may differ from a plain program's by a relative error of at most 0.022.
Values are sent between devices in bfloat16 or wider.
A program may use at most 768 MiB of HBM per device.

v0:
```python
import jax
import jax.numpy as jnp
from jax import lax
from jax.sharding import PartitionSpec as P

NAMES = ("w_gate", "w_up", "w_down")


def matmul(a, w):
    return jnp.dot(a, w, preferred_element_type=jnp.float32).astype(jnp.bfloat16)


def normed(h):
    wide = h.astype(jnp.float32)
    scale = lax.rsqrt(jnp.mean(wide**2, -1, keepdims=True) + 1e-6)
    return (wide * scale).astype(jnp.bfloat16)


def layer(h, w):
    a = normed(h)
    gate = jnp.dot(a, w["w_gate"], preferred_element_type=jnp.float32)
    up = jnp.dot(a, w["w_up"], preferred_element_type=jnp.float32)
    return h + matmul((jax.nn.silu(gate) * up).astype(jnp.bfloat16), w["w_down"])


def adamw(w, m, v, g):
    m = 0.9 * m + 0.1 * g
    v = 0.95 * v + 0.05 * g * g
    step = m * lax.rsqrt(v + 1e-8) + 0.1 * w
    return (w - 0.02 * step).astype(jnp.bfloat16), m, v


def solution(mesh):
    def step(x, dy, *arrays):
        weights, m, v = (arrays[i : i + 3] for i in (0, 3, 6))
        layers = weights[0].shape[0]
        h, kept = x[0], []
        for number in range(layers):
            kept.append(h)
            h = layer(h, {name: w[number] for name, w in zip(NAMES, weights, strict=True)})
        by_h, summed = dy[0], [None] * layers
        for number in reversed(range(layers)):
            _, back = jax.vjp(lambda w, h: layer(h, w), {name: w[number] for name, w in zip(NAMES, weights, strict=True)}, kept[number])
            by_w, by_h = back(by_h)
            summed[number] = [lax.psum(by_w[name], "dp") for name in NAMES]
        gradients = [jnp.stack([summed[number][i] for number in range(layers)]).astype(jnp.float32) for i in range(3)]
        new = [adamw(w.astype(jnp.float32), m, v, g) for w, m, v, g in zip(weights, m, v, gradients, strict=True)]
        return tuple(one[which] for which in range(3) for one in new)

    return jax.shard_map(
        step,
        mesh=mesh,
        in_specs=(P(("rep", "dp"), None, None),) * 2 + (P(None, None, None),) * 9,
        out_specs=(P("rep", None, None),) * 9,
        check_vma=False,
    )
```

profile of v0, /device:TPU:112, one launch (start us, length us, event | category | flops | bytes accessed | tf_op | source)
XLA Modules:
  0.0 1025.2 jit_solution(742536199580219666)
XLA Ops:
  7.2 0.1 all-reduce.3.cloned.1.call-start
  7.3 2.9 copy.20
  10.1 0.0 copy-start.1
  10.1 0.5 fusion.66
  10.6 0.0 slice-start.4
  10.6 4.2 copy.21
  14.8 12.5 %convolution_convert_fusion.4 = bf16[1024,3200]{1,0:T(8,128)(2,1)} fusion(bf16[2,3200,1024]{2,1,0:T(8,128)(2,1)} %param.15, bf16[1,1024,1024]{2,1,0:T(8,128)(2,1)} %param.12), kind=kOutput, calls=%fused_computation.59 | convolution fusion | flops 6714163200 | bytes 15204352 | tf_op jit(solution)/shard_map/transpose(jvp())/dot_general | solution.py:10
  27.4 0.0 slice-done.4
  27.4 0.0 slice-done.5
  27.4 0.0 slice-done.6
  27.4 0.0 slice-done.7
  27.4 0.0 copy-done.5
  27.4 10.5 %fusion.46 = f32[1024,3200]{1,0:T(8,128)} fusion(bf16[2,1024,3200]{2,1,0:T(8,128)(2,1)S(1)} %bitcast.77, bf16[1,1024,1024]{2,1,0:T(8,128)(2,1)S(1)} %copy-done.5, f32[1024]{0:T(1024)S(1)} %add_rsqrt_fusion), kind=kOutput, calls=%fused_computation.77 | convolution fusion | flops 6714032128 | bytes 21762048 | tf_op jit(solution)/shard_map/dot_general | solution.py:21
  37.8 0.0 copy-done.9
  37.9 16.7 %multiply_convert_fusion.1 = (bf16[1024,3200]{1,0:T(8,128)(2,1)}, f32[1024,3200]{1,0:T(8,128)}) fusion(f32[1024,3200]{1,0:T(8,128)} %fusion.46, bf16[2,1024,3200]{2,1,0:T(8,128)(2,1)} %param.14, bf16[1,1024,1024]{2,1,0:T(8,128)(2,1)} %param.11, f32[1024]{0:T(1024)S(1)} %add_rsqrt_fusion), kind=kOutput, calls=%fused_computation.47 | convolution fusion | flops 6733692928 | bytes 41422848 | tf_op jit(solution)/shard_map/dot_general | solution.py:22
  54.6 0.0 copy-done.1
  54.6 11.7 %fusion.70 = (f32[1024]{0:T(1024)S(1)}, bf16[1024,1024]{0,1:T(8,128)(2,1)S(1)}) fusion(bf16[1024,3200]{1,0:T(8,128)(2,1)} %get-tuple-element.24, bf16[2,3200,1024]{2,1,0:T(8,128)(2,1)} %param.15, bf16[1,1024,1024]{1,2,0:T(8,128)(2,1)S(1)} %copy.20), kind=kOutput, calls=%fused_computation.102 | convolution fusion | flops 6716128256 | bytes 17305600 | tf_op jit(solution)/shard_map/dot_general | solution.py:10
  66.3 0.0 copy-start.3
  66.3 0.0 copy-start.7
  66.3 1.3 copy-done.3
  67.6 13.2 %fusion.33 = f32[1024,3200]{1,0:T(8,128)} fusion(bf16[2,1024,3200]{2,1,0:T(8,128)(2,1)} %param.14, bf16[1024,1024]{0,1:T(8,128)(2,1)S(1)} %get-tuple-element.27, f32[1024]{0:T(1024)S(1)} %fusion.90), kind=kOutput, calls=%fused_computation.64 | convolution fusion | flops 6714032128 | bytes 21762048 | tf_op jit(solution)/shard_map/jvp()/dot_general | solution.py:22
  80.8 23.7 %fusion.17 = (bf16[1024,3200]{1,0:T(8,128)(2,1)}, f32[1024,3200]{1,0:T(8,128)}) fusion(f32[1024,3200]{1,0:T(8,128)} %fusion.33, bf16[1024,3200]{1,0:T(8,128)(2,1)} %convolution_convert_fusion.4, bf16[2,1024,3200]{2,1,0:T(8,128)(2,1)} %param.13, bf16[1024,1024]{0,1:T(8,128)(2,1)} %copy-done.3, f32[1024]{0:T(1024)S(1)} %fusion.90), kind=kOutput, calls=%fused_computation.35 | convolution fusion | flops 6753353728 | bytes 47976448 | tf_op jit(solution)/shard_map/jvp()/dot_general | solution.py:21
  104.5 0.0 copy-done.7
  104.5 13.5 %fusion.27 = bf16[1024,1024]{0,1:T(8,128)(2,1)S(1)} fusion(bf16[1024,3200]{1,0:T(8,128)(2,1)} %convolution_convert_fusion.4, bf16[2,1024,3200]{2,1,0:T(8,128)(2,1)} %param.14, f32[1024,3200]{1,0:T(8,128)} %get-tuple-element.29), kind=kOutput, calls=%fused_computation.51 | convolution fusion | flops 6730547200 | bytes 28311552 | tf_op jit(solution)/shard_map/transpose(jvp())/dot_general | solution.py:22
  118.0 0.0 copy-done.4
  118.0 0.0 copy-start.6
  118.0 14.3 %fusion.59 = bf16[1,1024,3200]{2,1,0:T(8,128)(2,1)} fusion(bf16[1024,3200]{1,0:T(8,128)(2,1)} %convolution_convert_fusion.4, bf16[1024,1024]{0,1:T(8,128)(2,1)S(1)} %copy-done.4, f32[1024]{0:T(1024)S(1)} %fusion.90, f32[1024,3200]{1,0:T(8,128)} %get-tuple-element.29), kind=kOutput, calls=%fused_computation.88 | convolution fusion | flops 6736969728 | bytes 28315648 | tf_op jit(solution)/shard_map/transpose(jvp())/dot_general | solution.py:22
  132.4 0.0 copy-done.6
  132.4 14.7 %fusion.54 = bf16[1,3200,1024]{2,1,0:T(8,128)(2,1)} fusion(f32[1024,3200]{1,0:T(8,128)} %fusion.33, bf16[1,1024,1024]{2,1,0:T(8,128)(2,1)S(1)} %copy-done.6, f32[1024,3200]{1,0:T(8,128)} %get-tuple-element.29), kind=kOutput, calls=%fused_computation.85 | convolution fusion | flops 6733824000 | bytes 34865152 | tf_op jit(solution)/shard_map/transpose(jvp())/dot_general | solution.py:10
  147.1 12.1 %fusion.52 = bf16[1,1024,3200]{2,1,0:T(8,128)(2,1)} fusion(bf16[1024,3200]{1,0:T(8,128)(2,1)} %get-tuple-element.28, bf16[1024,1024]{0,1:T(8,128)(2,1)S(1)} %copy-done.4, f32[1024]{0:T(1024)S(1)} %fusion.90), kind=kOutput, calls=%fused_computation.83 | convolution fusion | flops 6714032128 | bytes 15208448 | tf_op jit(solution)/shard_map/transpose(jvp())/dot_general | solution.py:21
  159.1 11.9 %fusion.72 = (f32[1024]{0:T(1024)S(1)}, bf16[1024,1024]{0,1:T(8,128)(2,1)S(1)}) fusion(bf16[1024,1024]{0,1:T(8,128)(2,1)S(1)} %copy-done.4, bf16[1024,1024]{0,1:T(8,128)(2,1)S(1)} %fusion.27, bf16[1024,3200]{1,0:T(8,128)(2,1)} %get-tuple-element.28, bf16[2,1024,3200]{2,1,0:T(8,128)(2,1)} %param.13), kind=kOutput, calls=%fused_computation.104 | convolution fusion | flops 6716128256 | bytes 19402752 | tf_op jit(solution)/shard_map/transpose(jvp())/dot_general | solution.py:21
  171.0 0.0 copy-done.8
  171.0 0.0 copy-done
  171.1 1.6 fusion.75
  172.6 0.0 slice-done
  172.6 0.0 slice-done.1
  172.6 0.0 slice-done.2
  172.7 0.0 slice-done.3
  172.7 9.3 convolution_convert_fusion.3
  182.0 12.0 %fusion.53 = bf16[1,3200,1024]{2,1,0:T(8,128)(2,1)} fusion(bf16[1024,3200]{1,0:T(8,128)(2,1)} %get-tuple-element.24, bf16[1024,1024]{0,1:T(8,128)(2,1)S(1)} %fusion.75), kind=kOutput, calls=%fused_computation.84 | convolution fusion | flops 6714163200 | bytes 15204352 | tf_op jit(solution)/shard_map/transpose(jvp())/dot_general | solution.py:10
  194.1 0.0 copy-done.2
  194.1 0.0 copy-done.10
  194.1 13.3 %fusion.55 = bf16[1,1024,3200]{2,1,0:T(8,128)(2,1)} fusion(bf16[1024,3200]{1,0:T(8,128)(2,1)S(1)} %copy-done.11, f32[1024,3200]{1,0:T(8,128)} %fusion.46, bf16[1,1024,1024]{1,2,0:T(8,128)(2,1)S(1)} %copy-done.2, f32[1024]{0:T(1024)S(1)} %copy-done.10), kind=kOutput, calls=%fused_computation.86 | convolution fusion | flops 6736969728 | bytes 28315648 | tf_op jit(solution)/shard_map/transpose(jvp())/dot_general | solution.py:22
  207.4 16.5 %fusion.56 = bf16[1,1024,3200]{2,1,0:T(8,128)(2,1)} fusion(f32[1024,3200]{1,0:T(8,128)} %fusion.46, f32[1024,3200]{1,0:T(8,128)} %get-tuple-element.25, bf16[1024,3200]{1,0:T(8,128)(2,1)} %convolution_convert_fusion.3, bf16[1,1024,1024]{1,2,0:T(8,128)(2,1)S(1)} %copy-done.2, f32[1024]{0:T(1024)S(1)} %copy-done.10), kind=kOutput, calls=%fused_computation.87 | convolution fusion | flops 6753353728 | bytes 41422848 | tf_op jit(solution)/shard_map/transpose(jvp())/dot_general | solution.py:21
  223.9 0.1 all-reduce.3.cloned.1.call-update
  223.9 652.7 %all-reduce.3.cloned.1.call-done = (bf16[1,1024,3200]{2,1,0:T(8,128)(2,1)}, bf16[1,1024,3200]{2,1,0:T(8,128)(2,1)}, bf16[1,1024,3200]{2,1,0:T(8,128)(2,1)}, bf16...) async-done(((bf16[1,1024,3200]{2,1,0:T(8,128)(2,1)}, bf16[1,1024,3200]{2,1,0:T(8,128)(2,1)}, ...) | async-done | bytes 39321616 | tf_op jit(solution)/shard_map/psum | solution.py:45
  876.6 49.5 %fusion.10 = (bf16[2,3200,1024]{2,1,0:T(8,128)(2,1)}, f32[2,3200,1024]{2,1,0:T(8,128)}, f32[2,3200,1024]{2,1,0:T(8,128)}) fusion(bf16[2,3200,1024]{2,1,0:T(8,128)(2,1)} %param.15, bf16[1,3200,1024]{2,1,0:T(8,128)(2,1)} %get-tuple-element.13, bf16[1,3200,1024]{2,1,0:T(8,128)(2,1)} %get-tuple-element.14, f32[2,3200,1024]{2,1,0:T(8,128)} %param.21, ...), kind=kLoop, calls=%fused_computation.22 | loop fusion | flops 124518400 | bytes 144179200 | tf_op jit(solution)/shard_map/convert_element_type | solution.py:30
  926.1 92.1 %fusion.2 = (bf16[2,1024,3200]{2,1,0:T(8,128)(2,1)}, f32[2,1024,3200]{2,1,0:T(8,128)}, f32[2,1024,3200]{2,1,0:T(8,128)}, bf16[2,1024,3200]{2,1,0:T(8,128)(2,1)},...) fusion(bf16[2,1024,3200]{2,1,0:T(8,128)(2,1)} %param.13, bf16[1,1024,3200]{2,1,0:T(8,128)(2,1)} %get-tuple-element.9, ...), kind=kLoop, calls=%fused_computation.14 | loop fusion | flops 249036800 | bytes 288358400 | tf_op jit(solution)/shard_map/convert_element_type | solution.py:30
  (21 shorter events, 0.1 us)
Async XLA Ops:
  7.2 869.4 %all-reduce.3.cloned.1.call-start = ((), (), s32[]{:S(2)}) async-start(), calls=%async_computation | async-start | bytes 78643200 | tf_op jit(solution)/shard_map/psum | solution.py:45
  10.1 44.4 %copy-start.1 = (bf16[1,1024,1024]{1,2,0:T(8,128)(2,1)}, bf16[1,1024,1024]{1,2,0:T(8,128)(2,1)S(1)}, u32[]{:S(2)}) copy-start(bf16[1,1024,1024]{1,2,0:T(8,128)(2,1)S(1)} %copy.20) | copy-start | bytes 6291460
  10.6 27.2 %copy-start.9 = (f32[1024]{0:T(1024)}, f32[1024]{0:T(1024)S(1)}, u32[]{:S(2)}) copy-start(f32[1024]{0:T(1024)S(1)} %add_rsqrt_fusion) | copy-start | bytes 12292
  10.6 16.7 %slice-start.4 = ((s8[13107200]{0:T(1024)(128)(4,1)}), s8[524288]{0:T(1024)(128)(4,1)S(1)}, s32[]{:S(2)}) async-start(s8[13107200]{0:T(1024)(128)(4,1)} %bitcast.76), calls=%async_computation.5 | async-start | bytes 1048576
  14.8 12.5 %slice-start.5 = ((s8[13107200]{0:T(1024)(128)(4,1)}), s8[4194304]{0:T(1024)(128)(4,1)S(1)}, s32[]{:S(2)}) async-start(s8[13107200]{0:T(1024)(128)(4,1)} %bitcast.76), calls=%async_computation.6 | async-start | bytes 8388608
  14.8 12.5 %slice-start.6 = ((s8[13107200]{0:T(1024)(128)(4,1)}), s8[4194304]{0:T(1024)(128)(4,1)S(1)}, s32[]{:S(2)}) async-start(s8[13107200]{0:T(1024)(128)(4,1)} %bitcast.76), calls=%async_computation.7 | async-start | bytes 8388608
  14.8 12.5 %slice-start.7 = ((s8[13107200]{0:T(1024)(128)(4,1)}), s8[4194304]{0:T(1024)(128)(4,1)S(1)}, s32[]{:S(2)}) async-start(s8[13107200]{0:T(1024)(128)(4,1)} %bitcast.76), calls=%async_computation.8 | async-start | bytes 8388608
  14.8 12.5 %copy-start.5 = (bf16[1,1024,1024]{2,1,0:T(8,128)(2,1)S(1)}, bf16[1,1024,1024]{2,1,0:T(8,128)(2,1)}, u32[]{:S(2)}) copy-start(bf16[1,1024,1024]{2,1,0:T(8,128)(2,1)} %param.11) | copy-start | bytes 6291460
  66.3 1.3 copy-start.3
  66.3 38.2 %copy-start.7 = (f32[1024]{0:T(1024)}, f32[1024]{0:T(1024)S(1)}, u32[]{:S(2)}) copy-start(f32[1024]{0:T(1024)S(1)} %get-tuple-element.26) | copy-start | bytes 12292
  104.5 13.5 %copy-start.4 = (bf16[1024,1024]{0,1:T(8,128)(2,1)S(1)}, bf16[1024,1024]{0,1:T(8,128)(2,1)}, u32[]{:S(2)}) copy-start(bf16[1024,1024]{0,1:T(8,128)(2,1)} %copy-done.3) | copy-start | bytes 6291460
  118.0 14.3 %copy-start.6 = (bf16[1,1024,1024]{2,1,0:T(8,128)(2,1)S(1)}, bf16[1,1024,1024]{2,1,0:T(8,128)(2,1)}, u32[]{:S(2)}) copy-start(bf16[1,1024,1024]{2,1,0:T(8,128)(2,1)} %param.12) | copy-start | bytes 6291460
  147.1 25.6 %slice-start = ((s8[13107200]{0:T(1024)(128)(4,1)}), s8[4194304]{0:T(1024)(128)(4,1)S(1)}, s32[]{:S(2)}) async-start(s8[13107200]{0:T(1024)(128)(4,1)} %bitcast.74), calls=%async_computation.1 | async-start | bytes 8388608
  147.1 25.6 %slice-start.1 = ((s8[13107200]{0:T(1024)(128)(4,1)}), s8[4194304]{0:T(1024)(128)(4,1)S(1)}, s32[]{:S(2)}) async-start(s8[13107200]{0:T(1024)(128)(4,1)} %bitcast.74), calls=%async_computation.2 | async-start | bytes 8388608
  147.1 25.6 %slice-start.2 = ((s8[13107200]{0:T(1024)(128)(4,1)}), s8[4194304]{0:T(1024)(128)(4,1)S(1)}, s32[]{:S(2)}) async-start(s8[13107200]{0:T(1024)(128)(4,1)} %bitcast.74), calls=%async_computation.3 | async-start | bytes 8388608
  159.1 11.9 %copy-start.8 = (f32[1024]{0:T(1024)S(1)}, f32[1024]{0:T(1024)}, u32[]{:S(2)}) copy-start(f32[1024]{0:T(1024)} %copy-done.7) | copy-start | bytes 12292
  159.1 11.9 %copy-start = (bf16[1,1024,1024]{1,2,0:T(8,128)(2,1)S(1)}, bf16[1,1024,1024]{1,2,0:T(8,128)(2,1)}, u32[]{:S(2)}) copy-start(bf16[1,1024,1024]{1,2,0:T(8,128)(2,1)} %copy.21) | copy-start | bytes 6291460
  159.1 13.5 %slice-start.3 = ((s8[13107200]{0:T(1024)(128)(4,1)}), s8[524288]{0:T(1024)(128)(4,1)S(1)}, s32[]{:S(2)}) async-start(s8[13107200]{0:T(1024)(128)(4,1)} %bitcast.74), calls=%async_computation.4 | async-start | bytes 1048576
  182.0 12.0 %copy-start.2 = (bf16[1,1024,1024]{1,2,0:T(8,128)(2,1)S(1)}, bf16[1,1024,1024]{1,2,0:T(8,128)(2,1)}, u32[]{:S(2)}) copy-start(bf16[1,1024,1024]{1,2,0:T(8,128)(2,1)} %copy-done.1) | copy-start | bytes 6291460
  182.0 12.0 %copy-start.10 = (f32[1024]{0:T(1024)S(1)}, f32[1024]{0:T(1024)}, u32[]{:S(2)}) copy-start(f32[1024]{0:T(1024)} %copy-done.9) | copy-start | bytes 12292
  182.0 12.0 %copy-start.11 = (bf16[1024,3200]{1,0:T(8,128)(2,1)S(1)}, bf16[1024,3200]{1,0:T(8,128)(2,1)}, u32[]{:S(2)}) copy-start(bf16[1024,3200]{1,0:T(8,128)(2,1)} %convolution_convert_fusion.3) | copy-start | bytes 19660804
Sparse Core Ops, SparseCore 0:
  224.0 652.5 all-reduce.2
where the time goes:
time: 1030 us
  waiting for transfers between devices  653 us (63%)
  matrix products  206 us (20%)
  other arithmetic  144 us (14%)
  between operations  14.5 us (1%)
    psum x1, waiting for transfers between devices, step(): summed[number] = [lax.psum(by_w[name], 'dp') for name in NAMES]  653 us
    convert_element_type x2, other arithmetic, adamw(): return ((w - 0.02 * step).astype(jnp.bfloat16), m, v)  142 us
    dot_general x5, matrix products, layer(): gate = jnp.dot(a, w['w_gate'], preferred_element_type=jnp.float32)  74.6 us
    dot_general x5, matrix products, layer(): up = jnp.dot(a, w['w_up'], preferred_element_type=jnp.float32)  71.1 us
    dot_general x5, matrix products, matmul(): jnp.dot(a, w, preferred_element_type=jnp.float32).astype(jnp.bfloat16)  60.3 us
  transfers between devices with their start and end apart: 1, of which 1 were waited for; matrix products, arithmetic and copies ran while one was open for 0% of the time, Pallas kernels for 0%

commit v1 on v0

v1 whole, which is shorter than its diff:
```python
import functools

import jax
import jax.numpy as jnp
from jax import lax
from jax.experimental import pallas as pl
from jax.experimental.pallas import tpu as pltpu
from jax.sharding import PartitionSpec as P

F32, BF16 = jnp.float32, jnp.bfloat16
NT = (((1,), (1,)), ((), ()))


def adam_store(g, w, m_ref, v_ref, w_out, m_out, v_out):
    m = 0.9 * m_ref[0] + 0.1 * g
    v = 0.95 * v_ref[0] + 0.05 * g * g
    w_out[0] = (w - 0.02 * (m * lax.rsqrt(v + 1e-8) + 0.1 * w)).astype(BF16)
    m_out[0] = m
    v_out[0] = v


def kernel(parts, chunk, n_out, aliased, a, dh, wg, wu, wd, mg, mu, md, vg, vu, vd, *rest):
    rest = rest[aliased:]
    wgo, wuo, wdo, mgo, muo, mdo, vgo, vuo, vdo, wgt, wut, hid, dgt, dut = rest
    s = pl.program_id(1)
    tokens = a.shape[0] // parts

    @pl.when(s == 0)
    def _():
        wgt[...] = wg[0].T
        wut[...] = wu[0].T

    @pl.when(s < parts)
    def _():
        def one(i, _):
            rows = pl.ds(pl.multiple_of(s * tokens + i * chunk, chunk), chunk)
            ac, dc = a[rows, :], dh[rows, :]
            g = lax.dot_general(wgt[...], ac, NT, preferred_element_type=F32)
            u = lax.dot_general(wut[...], ac, NT, preferred_element_type=F32)
            d = lax.dot_general(wd[0], dc, NT, preferred_element_type=F32).astype(BF16).astype(F32)
            sig = 1.0 / (1.0 + jnp.exp(-g))
            silu = g * sig
            hid[:, rows] = (silu * u).astype(BF16)
            dut[:, rows] = (d * silu).astype(BF16)
            dgt[:, rows] = (d * u * (sig + silu * (1.0 - sig))).astype(BF16)
            return 0

        lax.fori_loop(0, tokens // chunk, one, 0)

    @pl.when(s >= parts)
    def _():
        n = pl.multiple_of((s - parts) * n_out, n_out)
        cols = pl.ds(n, n_out)
        ac, dc = a[:, cols], dh[:, cols]
        g = jnp.dot(dgt[...], ac, preferred_element_type=F32)
        adam_store(g.T.astype(BF16).astype(F32), wg[0, cols, :].astype(F32), mg, vg, wgo, mgo, vgo)
        g = jnp.dot(dut[...], ac, preferred_element_type=F32)
        adam_store(g.T.astype(BF16).astype(F32), wu[0, cols, :].astype(F32), mu, vu, wuo, muo, vuo)
        g = jnp.dot(hid[...], dc, preferred_element_type=F32)
        adam_store(g.astype(BF16).astype(F32), wd[0, :, cols].astype(F32), md, vd, wdo, mdo, vdo)


def layer_step(number, a, dh, w, m, v, done=None, ffb=640, parts=2, chunk=512, n_out=256):
    rows, d = a.shape
    ff = w[0].shape[2]
    chunks = d // n_out
    late = lambda s: jnp.maximum(s - parts, 0)
    whole = pl.BlockSpec((rows, d), lambda f, s: (0, 0), pipeline_mode=pl.Buffered(1))
    w_in = [pl.BlockSpec((1, d, ffb), lambda f, s: (number, 0, f))] * 2 + [pl.BlockSpec((1, ffb, d), lambda f, s: (number, f, 0))]
    tile = [pl.BlockSpec((1, n_out, ffb), lambda f, s: (number, late(s), f))] * 2 + [
        pl.BlockSpec((1, ffb, n_out), lambda f, s: (number, f, late(s)))
    ]
    out_shape = [jax.ShapeDtypeStruct(x.shape, x.dtype) for x in (*w, *m, *v)]
    extra = list(done) if done is not None else []
    return pl.pallas_call(
        functools.partial(kernel, parts, chunk, n_out, len(extra)),
        grid=(ff // ffb, parts + chunks),
        in_specs=[whole, whole] + w_in + tile + tile + [pl.BlockSpec(memory_space=pl.ANY)] * len(extra),
        out_specs=tile * 3,
        out_shape=out_shape,
        scratch_shapes=[pltpu.VMEM((ffb, d), BF16)] * 2 + [pltpu.VMEM((ffb, rows), BF16)] * 3,
        input_output_aliases={11 + i: i for i in range(len(extra))},
        compiler_params=pltpu.CompilerParams(vmem_limit_bytes=67_043_328, dimension_semantics=("arbitrary", "arbitrary")),
        cost_estimate=pl.CostEstimate(flops=12 * rows * d * ff, bytes_accessed=20 * 3 * d * ff, transcendentals=0),
        name=f"layer_step_{number}",
    )(a, dh, *w, *m, *v, *extra)


def matmul(a, w):
    return jnp.dot(a, w, preferred_element_type=F32).astype(BF16)


def matmul_t(a, w):
    return lax.dot_general(a, w, NT, preferred_element_type=F32).astype(BF16)


def scale_of(h):
    wide = h.astype(F32)
    return lax.rsqrt(jnp.mean(wide**2, -1, keepdims=True) + 1e-6)


def own_chain(x, dy, w):
    (gate0, gate1), (up0, up1), (down0, down1) = w
    a0 = (x.astype(F32) * scale_of(x)).astype(BF16)
    g, u = jnp.dot(a0, gate0, preferred_element_type=F32), jnp.dot(a0, up0, preferred_element_type=F32)
    h = x + matmul((jax.nn.silu(g) * u).astype(BF16), down0)
    scale = scale_of(h)
    wide = h.astype(F32)
    a1 = (wide * scale).astype(BF16)
    return a0, h, a1, scale


def own_back(h, a, scale, dy, gate, up, down):
    g, u = jnp.dot(a, gate, preferred_element_type=F32), jnp.dot(a, up, preferred_element_type=F32)
    d = matmul_t(dy, down).astype(F32)
    sig = jax.nn.sigmoid(g)
    silu = g * sig
    da = matmul_t((d * u * (sig + silu * (1.0 - sig))).astype(BF16), gate) + matmul_t((d * silu).astype(BF16), up)
    wide, da = h.astype(F32), da.astype(F32)
    back = da * scale - wide * (scale * scale * scale) * jnp.mean(da * wide, -1, keepdims=True)
    return dy + back.astype(BF16)


def solution(mesh):
    def step(x, dy, *arrays):
        w, m, v = (arrays[i : i + 3] for i in (0, 3, 6))
        x, dy = x[0], dy[0]
        gather = lambda one: lax.all_gather(one, "dp", tiled=True)
        pairs = tuple((one[0], one[1]) for one in w)
        a0, h1, a1, scale = own_chain(x, dy, pairs)
        dy_all = gather(dy)
        a1_all = gather(a1)
        a0, _ = lax.optimization_barrier((a0, a1))
        a0_all = gather(a0)
        dh1 = own_back(h1, a1, scale, dy, *(one[1] for one in w))
        dh1_all = gather(dh1)
        new = layer_step(1, a1_all, dy_all, w, m, v)
        return tuple(layer_step(0, a0_all, dh1_all, w, m, v, done=new))

    return jax.shard_map(
        step,
        mesh=mesh,
        in_specs=(P(("rep", "dp"), None, None),) * 2 + (P(None, None, None),) * 9,
        out_specs=(P("rep", None, None),) * 9,
        check_vma=False,
    )
```

time: 1030 us -> 634 us (0.62)
  waiting for transfers between devices: 653 us -> 52.1 us
  Pallas kernels: 0 us -> 445 us
  other arithmetic: 144 us -> 11.2 us
  matrix products: 206 us -> 103 us
    psum x1 -> x0, waiting for transfers between devices: 653 us -> none  [step(): summed[number] = [lax.psum(by_w[name], 'dp') for name in NAMES]]
    pallas_call x0 -> x2, Pallas kernels: none -> 445 us  [layer_step(): pl.pallas_call(functools.partial(kernel, parts, chunk, n_out, len(extra))...]
    convert_element_type x2, other arithmetic: 142 us -> 5.08 us  [the longest x1 3.35 us: own_chain(): a0 = (x.astype(F32) * scale_of(x)).astype(BF16)]
    dot_general x15 -> x6, matrix products: 206 us -> 103 us  [the longest x3 52.1 us: matmul_t(): return lax.dot_general(a, w, NT, preferred_element_type=F32).astype(BF16)]
    all_gather x0 -> x4, waiting for transfers between devices: none -> 51.2 us  [step(): gather = lambda one: lax.all_gather(one, 'dp', tiled=True)]
  transfers between devices with their start and end apart: 1 -> 4, of which waited for: 1 -> 1; matrix products, arithmetic and copies ran while one was open for 0% -> 18% of each run, Pallas kernels for 0% -> 36%
where the time goes in v1:
time: 634 us; the launch traced here: 626 us
  Pallas kernels  445 us (70%)
  matrix products  103 us (16%)
  waiting for transfers between devices  52.1 us (8%)
  between operations  14.3 us (2%)
  other arithmetic  11.2 us (2%)
    pallas_call x2, Pallas kernels, layer_step(): pl.pallas_call(functools.partial(kernel, parts, chunk, n_out, len(extra))...  445 us
    dot_general x3, matrix products, matmul_t(): return lax.dot_general(a, w, NT, preferred_element_type=F32).astype(BF16)  52.1 us
    all_gather x4, waiting for transfers between devices, step(): gather = lambda one: lax.all_gather(one, 'dp', tiled=True)  51.2 us
    dot_general x1, matrix products, matmul(): return jnp.dot(a, w, preferred_element_type=F32).astype(BF16)  24.2 us
    dot_general x1, matrix products, own_chain(): jnp.dot(a0, gate0, preferred_element_type=F32)  13.6 us
    dot_general x1, matrix products, own_back(): jnp.dot(a, gate, preferred_element_type=F32)  13.1 us
  transfers between devices with their start and end apart: 4, of which 1 were waited for; matrix products, arithmetic and copies ran while one was open for 18% of the time, Pallas kernels for 36%

profile of v1, /device:TPU:112, one launch (start us, length us, event | category | flops | bytes accessed | tf_op | source)
XLA Modules:
  0.0 626.2 jit_solution(15633305926298147376)
XLA Ops:
  7.2 0.1 all-gather.12.cloned.1.call-start
  7.3 0.7 all-gather.12.cloned.1.call-update
  8.0 0.1 all-gather.10.cloned.1.call-start
  8.1 2.1 fusion.32
  10.1 13.6 %fusion.17 = f32[1024,3200]{1,0:T(8,128)} fusion(bf16[2,1024,3200]{2,1,0:T(8,128)(2,1)} %wg.3, bf16[1,1024,1024]{2,1,0:T(8,128)(2,1)} %param.11, f32[1024]{0:T(1024)S(1)} %add_rsqrt_fusion.1), kind=kOutput, calls=%fused_computation.24 | convolution fusion | flops 6714032128 | bytes 21762048 | tf_op jit(solution)/shard_map/dot_general | solution.py:105
  23.8 24.2 %fusion.36 = (f32[1024]{0:T(1024)S(1)}, bf16[1024,1024]{1,0:T(8,128)(2,1)S(1)}) fusion(bf16[2,3200,1024]{2,1,0:T(8,128)(2,1)} %wd.3, f32[1024,3200]{1,0:T(8,128)} %fusion.17, bf16[2,1024,3200]{2,1,0:T(8,128)(2,1)} %wu.3, bf16[1,1024,1024]{2,1,0:T(8,128)(2,1)} %param.11, f32[1024]{0:T(1024)S(1)} %add_rsqrt_fusion.1), kind=kOutput, calls=%fused_computation.43 | convolution fusion | flops 13452966912 | bytes 32514048 | tf_op jit(solution)/shard_map/dot_general | solution.py:90
  48.0 1.7 fusion.37
  49.7 0.1 all-gather.10.cloned.1.call-update
  49.8 0.1 all-gather.6.cloned.1.call-start
  49.8 3.3 fusion.33
  53.2 0.1 all-gather.6.cloned.1.call-update
  53.3 0.2 all-gather.8.cloned.1.call-start
  53.5 0.0 copy-start
  53.5 12.5 %convolution_convert_fusion = bf16[1024,3200]{1,0:T(8,128)(2,1)} fusion(bf16[2,3200,1024]{2,1,0:T(8,128)(2,1)} %wd.3, bf16[1,1024,1024]{2,1,0:T(8,128)(2,1)} %param.12), kind=kOutput, calls=%fused_computation.8 | convolution fusion | flops 6714163200 | bytes 15204352 | tf_op jit(solution)/shard_map/dot_general | solution.py:94
  66.0 0.0 copy-done
  66.0 13.1 %fusion.6 = f32[1024,3200]{1,0:T(8,128)} fusion(bf16[1024,1024]{1,0:T(8,128)(2,1)S(1)} %copy-done, bf16[2,1024,3200]{2,1,0:T(8,128)(2,1)} %wg.3), kind=kOutput, calls=%fused_computation.15 | convolution fusion | flops 6710886400 | bytes 21757952 | tf_op jit(solution)/shard_map/dot_general | solution.py:114
  79.1 22.9 %fusion.4 = bf16[1024,1024]{1,0:T(8,128)(2,1)} fusion(bf16[1024,3200]{1,0:T(8,128)(2,1)} %convolution_convert_fusion, f32[1024,3200]{1,0:T(8,128)} %fusion.6, bf16[1024,1024]{1,0:T(8,128)(2,1)} %fusion.37, bf16[2,1024,3200]{2,1,0:T(8,128)(2,1)} %wg.3, bf16[2,1024,3200]{2,1,0:T(8,128)(2,1)} %wu.3), kind=kOutput, calls=%fused_computation.13 | convolution fusion | flops 13457817600 | bytes 36962304 | tf_op jit(solution)/shard_map/dot_general | solution.py:94
  101.9 16.8 %fusion.39 = (f32[1024]{0:T(1024)S(1)}, bf16[1024,1024]{1,0:T(8,128)(2,1)}) fusion(bf16[1024,1024]{1,0:T(8,128)(2,1)S(1)} %get-tuple-element.32, bf16[1024,1024]{1,0:T(8,128)(2,1)} %fusion.4, bf16[2,1024,3200]{2,1,0:T(8,128)(2,1)} %wu.3, bf16[1024,3200]{1,0:T(8,128)(2,1)} %convolution_convert_fusion, f32[1024,3200]{1,0:T(8,128)} %fusion.6), kind=kOutput, calls=%fused_computation.46 | convolution fusion | flops 6740114432 | bytes 32509952 | tf_op jit(solution)/shard_map/dot_general | solution.py:94
  118.7 4.1 fusion.41
  122.8 0.1 all-gather.8.cloned.1.call-update
  122.9 0.0 all-gather.12.cloned.1.call-done
  122.9 51.1 %all-gather.10.cloned.1.call-done.a = bf16[4096,1024]{1,0:T(8,128)(2,1)} async-done(((bf16[1024,1024]{1,0:T(8,128)(2,1)}), bf16[4096,1024]{1,0:T(8,128)(2,1)}) %all-gather.10.cloned.1.call-update) | async-done | bytes 8388624 | tf_op jit(solution)/shard_map/all_gather | solution.py:128
  174.0 222.5 %layer_step_1.1 = (bf16[2,1024,3200]{2,1,0:T(8,128)(2,1)}, bf16[2,1024,3200]{2,1,0:T(8,128)(2,1)}, bf16[2,3200,1024]{2,1,0:T(8,128)(2,1)}, f32[2,1024,3200]{2,1,...) custom-call(bf16[4096,1024]{1,0:T(8,128)(2,1)} %all-gather.10.cloned, ...), custom_call_target="tpu_custom_call" | custom-call | flops 161061273600 | bytes 196608000 | tf_op jit(solution)/shard_map/layer_step_1/pallas_call | solution.py:75
  396.5 0.0 all-gather.6.cloned.1.call-done.a
  396.6 0.0 all-gather.8.cloned.1.call-done.dh
  396.6 222.6 %layer_step_0.1 = (bf16[2,1024,3200]{2,1,0:T(8,128)(2,1)}, bf16[2,1024,3200]{2,1,0:T(8,128)(2,1)}, bf16[2,3200,1024]{2,1,0:T(8,128)(2,1)}, f32[2,1024,3200]{2,1,...) custom-call(bf16[4096,1024]{1,0:T(8,128)(2,1)} %all-gather.6.cloned., ...), custom_call_target="tpu_custom_call", output_to_operand_aliasing={{0}: (11, {}), {1}: (12, {}), {2}: (13, {}), {3}: (14, {}),... | custom-call | flops 161061273600 | bytes 196608000 | tf_op jit(solution)/shard_map/layer_step_0/pallas_call | solution.py:75
  (3 shorter events, 0.0 us)
Async XLA Ops:
  7.2 115.7 %all-gather.12.cloned.1.call-start = ((), (), s32[]{:S(2)}) async-start(), calls=%async_computation.3 | async-start | bytes 10485760 | tf_op jit(solution)/shard_map/all_gather | solution.py:128
  8.0 166.1 %all-gather.10.cloned.1.call-start = ((), (), s32[]{:S(2)}) async-start(), calls=%async_computation.2 | async-start | bytes 10485760 | tf_op jit(solution)/shard_map/all_gather | solution.py:128
  49.8 346.8 %all-gather.6.cloned.1.call-start = ((), (), s32[]{:S(2)}) async-start(), calls=%async_computation | async-start | bytes 10485760 | tf_op jit(solution)/shard_map/all_gather | solution.py:128
  53.3 343.3 %all-gather.8.cloned.1.call-start = ((), (), s32[]{:S(2)}) async-start(), calls=%async_computation.1 | async-start | bytes 10485760 | tf_op jit(solution)/shard_map/all_gather | solution.py:128
  53.5 12.5 %copy-start = (bf16[1024,1024]{1,0:T(8,128)(2,1)S(1)}, bf16[1024,1024]{1,0:T(8,128)(2,1)}, u32[]{:S(2)}) copy-start(bf16[1024,1024]{1,0:T(8,128)(2,1)} %fusion.37) | copy-start | bytes 6291460
Sparse Core Ops, SparseCore 0:
  9.6 82.1 all-gather.11
  93.8 80.1 all-gather.9
  175.6 80.1 all-gather.5
  257.2 80.1 all-gather.7

commit v2 on v1

v2 whole, which is shorter than its diff:
```python
import functools

import jax
import jax.numpy as jnp
from jax import lax
from jax.experimental import pallas as pl
from jax.experimental.pallas import tpu as pltpu
from jax.sharding import PartitionSpec as P


F32, BF16 = jnp.float32, jnp.bfloat16
NT = (((1,), (1,)), ((), ()))
TN = (((0,), (0,)), ((), ()))


def adam_store(g, w, m_ref, v_ref, w_out, m_out, v_out):
    g = g.astype(BF16).astype(F32)
    m = 0.9 * m_ref[0] + 0.1 * g
    v = 0.95 * v_ref[0] + 0.05 * g * g
    w_out[0] = (w.astype(F32) - 0.02 * (m * lax.rsqrt(v + 1e-8) + 0.1 * w.astype(F32))).astype(BF16)
    m_out[0] = m
    v_out[0] = v


def layer_kernel(pieces, tokens, chunk, n_out, bases, extra, *refs):
    a_all, dh_all, wg, wu, wd, mg, mu, md, vg, vu, vd = refs[:11]
    base = refs[11 : 11 + bases]
    rest = refs[11 + bases + extra :]
    wgo, wuo, wdo, mgo, muo, mdo, vgo, vuo, vdo, a, dh, wgt, wut, hid, dgt, dut, sem = rest
    f, s = pl.program_id(0), pl.program_id(1)
    size = tokens
    a_at, dh_at = pieces

    def source(i):
        return pl.ds(pl.multiple_of(i * size, size), size)

    def copies(i):
        rows = pl.ds(pl.multiple_of(i * size, size), size)
        return (
            pltpu.make_async_copy(a_all.at[source(a_at(i))], a.at[rows], sem.at[0, i]),
            pltpu.make_async_copy(dh_all.at[source(dh_at(i))], dh.at[rows], sem.at[1, i]),
        )

    @pl.when((f == 0) & (s == 0))
    def _():
        for i in range(a.shape[0] // size):
            for copy in copies(i):
                copy.start()

    @pl.when(s == 0)
    def _():
        wgt[...] = wg[0].T
        wut[...] = wu[0].T

        def one(i, _):
            @pl.when((f == 0) & (lax.rem(i, size // chunk) == 0))
            def _():
                for copy in copies(lax.div(i, size // chunk)):
                    copy.wait()

            rows = pl.ds(pl.multiple_of(i * chunk, chunk), chunk)
            ac, dc = a[rows, :], dh[rows, :]
            g = lax.dot_general(wgt[...], ac, NT, preferred_element_type=F32)
            u = lax.dot_general(wut[...], ac, NT, preferred_element_type=F32)
            d = lax.dot_general(wd[0], dc, NT, preferred_element_type=F32).astype(BF16).astype(F32)
            sig = 1.0 / (1.0 + jnp.exp(-g))
            silu = g * sig
            hid[:, rows] = (silu * u).astype(BF16)
            dut[:, rows] = (d * silu).astype(BF16)
            dgt[:, rows] = (d * u * (sig + silu * (1.0 - sig))).astype(BF16)
            return 0

        lax.fori_loop(0, a.shape[0] // chunk, one, 0)

    @pl.when(s >= 1)
    def _():
        cols = pl.ds(pl.multiple_of((s - 1) * n_out, n_out), n_out)
        ac, dc = a[:, cols], dh[:, cols]
        g = jnp.dot(dgt[...], ac, preferred_element_type=F32).T
        adam_store(g + base[0][...] if bases else g, wg[0, cols, :], mg, vg, wgo, mgo, vgo)
        g = jnp.dot(dut[...], ac, preferred_element_type=F32).T
        adam_store(g + base[1][...] if bases else g, wu[0, cols, :], mu, vu, wuo, muo, vuo)
        g = jnp.dot(hid[...], dc, preferred_element_type=F32)
        adam_store(g + base[2][...] if bases else g, wd[0, :, cols], md, vd, wdo, mdo, vdo)


def layer_step(number, a, dh, pieces, w, m, v, done=None, base=None, skip=0, after=(), ffb=640, chunk=256, n_out=256):
    count, size, *maps = pieces
    d = a.shape[1]
    rows = count * size
    ff = w[0].shape[2] - skip * ffb
    chunks = d // n_out
    late = lambda s: jnp.maximum(s - 1, 0)
    apart = pl.BlockSpec(memory_space=pl.ANY)
    w_in = [pl.BlockSpec((1, d, ffb), lambda f, s: (number, 0, f + skip))] * 2 + [
        pl.BlockSpec((1, ffb, d), lambda f, s: (number, f + skip, 0))
    ]
    tile = [pl.BlockSpec((1, n_out, ffb), lambda f, s: (number, late(s), f + skip))] * 2 + [
        pl.BlockSpec((1, ffb, n_out), lambda f, s: (number, f + skip, late(s)))
    ]
    flat = [pl.BlockSpec((n_out, ffb), lambda f, s: (late(s), f))] * 2 + [pl.BlockSpec((ffb, n_out), lambda f, s: (f, late(s)))]
    out_shape = [jax.ShapeDtypeStruct(x.shape, x.dtype) for x in (*w, *m, *v)]
    base, extra, after = list(base or []), list(done or []), list(after)
    first = 11 + len(base)
    return pl.pallas_call(
        functools.partial(layer_kernel, maps, size, chunk, n_out, len(base), len(extra) + len(after)),
        grid=(ff // ffb, chunks + 1),
        in_specs=[apart] * 2 + w_in + tile + tile + flat[: len(base)] + [apart] * (len(extra) + len(after)),
        out_specs=tile * 3,
        out_shape=out_shape,
        scratch_shapes=[pltpu.VMEM((rows, d), BF16)] * 2
        + [pltpu.VMEM((ffb, d), BF16)] * 2
        + [pltpu.VMEM((ffb, rows), BF16)] * 3
        + [pltpu.SemaphoreType.DMA((2, count))],
        input_output_aliases={first + i: i for i in range(len(extra))},
        compiler_params=pltpu.CompilerParams(vmem_limit_bytes=67_043_328, dimension_semantics=("arbitrary", "arbitrary")),
        cost_estimate=pl.CostEstimate(flops=12 * rows * d * ff, bytes_accessed=20 * 3 * d * ff, transcendentals=0),
    )(a, dh, *w, *m, *v, *base, *extra, *after)


def part_kernel(chunk, n_out, a_all, dh_all, wgt, wut, wd, out, a, dh, hid, dgt, dut, sem):
    count = sem.shape[1]
    size = a.shape[0] // count

    def copies(i):
        rows = pl.ds(pl.multiple_of(i * size, size), size)
        return (
            pltpu.make_async_copy(a_all.at[rows], a.at[rows], sem.at[0, i]),
            pltpu.make_async_copy(dh_all.at[rows], dh.at[rows], sem.at[1, i]),
        )

    for i in range(count):
        for copy in copies(i):
            copy.start()

    def one(i, _):
        @pl.when(lax.rem(i, size // chunk) == 0)
        def _():
            for copy in copies(lax.div(i, size // chunk)):
                copy.wait()

        rows = pl.ds(pl.multiple_of(i * chunk, chunk), chunk)
        ac, dc = a[rows, :], dh[rows, :]
        g = lax.dot_general(wgt[...], ac, NT, preferred_element_type=F32)
        u = lax.dot_general(wut[...], ac, NT, preferred_element_type=F32)
        d = lax.dot_general(wd[...], dc, NT, preferred_element_type=F32).astype(BF16).astype(F32)
        sig = 1.0 / (1.0 + jnp.exp(-g))
        silu = g * sig
        hid[:, rows] = (silu * u).astype(BF16)
        dut[:, rows] = (d * silu).astype(BF16)
        dgt[:, rows] = (d * u * (sig + silu * (1.0 - sig))).astype(BF16)
        return 0

    lax.fori_loop(0, a.shape[0] // chunk, one, 0)
    each = wgt.shape[0]

    def two(i, _):
        cols = pl.ds(pl.multiple_of(i * n_out, n_out), n_out)
        ac, dc = a[:, cols], dh[:, cols]
        out[0:each, cols] = jnp.dot(dgt[...], ac, preferred_element_type=F32).astype(BF16)
        out[each : 2 * each, cols] = jnp.dot(dut[...], ac, preferred_element_type=F32).astype(BF16)
        out[2 * each : 3 * each, cols] = jnp.dot(hid[...], dc, preferred_element_type=F32).astype(BF16)
        return 0

    lax.fori_loop(0, a.shape[1] // n_out, two, 0)


def part_grads(a, dh, wgt, wut, wd, pieces, chunk=512, n_out=256):
    rows, d = a.shape
    each = wgt.shape[0]
    inside = pl.BlockSpec(memory_space=pltpu.VMEM)
    return pl.pallas_call(
        functools.partial(part_kernel, chunk, n_out),
        in_specs=[pl.BlockSpec(memory_space=pl.ANY)] * 2 + [inside] * 3,
        out_specs=inside,
        out_shape=jax.ShapeDtypeStruct((3 * each, d), BF16),
        scratch_shapes=[pltpu.VMEM((rows, d), BF16)] * 2 + [pltpu.VMEM((each, rows), BF16)] * 3 + [pltpu.SemaphoreType.DMA((2, pieces))],
        compiler_params=pltpu.CompilerParams(vmem_limit_bytes=67_043_328),
        cost_estimate=pl.CostEstimate(flops=12 * rows * d * each, bytes_accessed=4 * rows * d, transcendentals=0),
        name="part_grads",
    )(a, dh, wgt, wut, wd)


def update_kernel(extra, *refs):
    grads, (wg, wu, wd, mg, mu, md, vg, vu, vd), outs = refs[:6], refs[6:15], refs[15 + extra :]
    wgo, wuo, wdo, mgo, muo, mdo, vgo, vuo, vdo = outs
    g, u, d = (jnp.concatenate([grads[2 * i][...], grads[2 * i + 1][...]]).astype(F32) for i in range(3))
    adam_store(g.T, wg[0], mg, vg, wgo, mgo, vgo)
    adam_store(u.T, wu[0], mu, vu, wuo, muo, vuo)
    adam_store(d, wd[0], md, vd, wdo, mdo, vdo)


def update_step(number, grads, w, m, v, done, blocks, ffb=640, n_out=256):
    each, d = ffb // 2, grads.shape[1]
    parts = [pl.BlockSpec((each, n_out), lambda f, s, i=i, j=j: ((2 * f + j) * 3 + i, s)) for i in range(3) for j in range(2)]
    tile = [pl.BlockSpec((1, n_out, ffb), lambda f, s: (number, s, f))] * 2 + [pl.BlockSpec((1, ffb, n_out), lambda f, s: (number, f, s))]
    return pl.pallas_call(
        functools.partial(update_kernel, len(done)),
        grid=(blocks, d // n_out),
        in_specs=parts + tile * 3 + [pl.BlockSpec(memory_space=pl.ANY)] * len(done),
        out_specs=tile * 3,
        out_shape=[jax.ShapeDtypeStruct(x.shape, x.dtype) for x in (*w, *m, *v)],
        input_output_aliases={15 + i: i for i in range(len(done))},
        compiler_params=pltpu.CompilerParams(vmem_limit_bytes=67_043_328, dimension_semantics=("arbitrary", "arbitrary")),
        cost_estimate=pl.CostEstimate(flops=60 * blocks * d * ffb, bytes_accessed=66 * blocks * d * ffb, transcendentals=0),
    )(*[grads] * 6, *w, *m, *v, *done)


def matmul(a, w):
    return jnp.dot(a, w, preferred_element_type=F32).astype(BF16)


def matmul_t(a, w):
    return lax.dot_general(a, w, NT, preferred_element_type=F32).astype(BF16)


def scale_of(h):
    wide = h.astype(F32)
    return lax.rsqrt(jnp.mean(wide**2, -1, keepdims=True) + 1e-6)


def own_chain(x, w):
    (gate0, gate1), (up0, up1), (down0, down1) = w
    a0 = (x.astype(F32) * scale_of(x)).astype(BF16)
    g, u = jnp.dot(a0, gate0, preferred_element_type=F32), jnp.dot(a0, up0, preferred_element_type=F32)
    h = x + matmul((jax.nn.silu(g) * u).astype(BF16), down0)
    scale = scale_of(h)
    wide = h.astype(F32)
    a1 = (wide * scale).astype(BF16)
    return a0, h, a1, scale


def own_back(h, a, scale, dy, gate, up, down):
    g, u = jnp.dot(a, gate, preferred_element_type=F32), jnp.dot(a, up, preferred_element_type=F32)
    d = matmul_t(dy, down).astype(F32)
    sig = jax.nn.sigmoid(g)
    silu = g * sig
    dg, du, hidden = (d * u * (sig + silu * (1.0 - sig))).astype(BF16), (d * silu).astype(BF16), (silu * u).astype(BF16)
    da = matmul_t(dg, gate) + matmul_t(du, up)
    wide, da = h.astype(F32), da.astype(F32)
    back = da * scale - wide * (scale * scale * scale) * jnp.mean(da * wide, -1, keepdims=True)
    parts = [lax.dot_general(one, other, TN, preferred_element_type=F32) for one, other in ((a, dg), (a, du), (hidden, dy))]
    return dy + back.astype(BF16), parts


BLOCK, SHARED = 640, 2


def solution(mesh):
    n = mesh.shape["dp"]
    assert SHARED * BLOCK // n * 2 == BLOCK

    def step(x, dy, *arrays):
        w, m, v = (arrays[i : i + 3] for i in (0, 3, 6))
        x, dy = x[0], dy[0]

        def gather(one):
            return lax.all_gather(one, "dp", tiled=True)

        pairs = tuple((one[0], one[1]) for one in w)
        a0, h1, a1, scale = own_chain(x, pairs)
        dy_all = gather(dy)
        a1_all = gather(a1)
        dh1, parts = own_back(h1, a1, scale, dy, *(one[1] for one in w))
        a0, _ = lax.optimization_barrier((a0, a1))
        a0_all, dh1_all = gather(a0), gather(dh1)
        others = lambda i: lax.rem(lax.axis_index("dp") + 1 + i, n)
        each = SHARED * BLOCK // n
        start = lax.axis_index("dp") * each
        gate, up = (lax.dynamic_slice(one, (0, 0, start), (1, one.shape[1], each))[0].T for one in w[:2])
        down = lax.dynamic_slice(w[2], (0, start, 0), (1, each, w[2].shape[2]))[0]
        new = layer_step(1, a1_all, dy_all, (n - 1, x.shape[0], others, others), w, m, v, base=parts)
        a0_all, *new = lax.optimization_barrier((a0_all, *new))
        mine = part_grads(a0_all, dh1_all, gate, up, down, n)
        grads = gather(mine)
        whole = (n, x.shape[0], lambda i: i, lambda i: i)
        new = layer_step(0, a0_all, dh1_all, whole, w, m, v, done=new, skip=SHARED, after=(mine,))
        return tuple(update_step(0, grads, w, m, v, new, SHARED))

    return jax.shard_map(
        step,
        mesh=mesh,
        in_specs=(P(("rep", "dp"), None, None),) * 2 + (P(None, None, None),) * 9,
        out_specs=(P("rep", None, None),) * 9,
        check_vma=False,
    )
```

time: 634 us -> 574 us (0.905)
  Pallas kernels: 445 us -> 370 us
  matrix products: 103 us -> 159 us
  waiting for transfers between devices: 52.1 us -> 1 us
  local copies, waits for them, and re-layouts: 0.01 us -> 9.37 us
    pallas_call x2 -> x4, Pallas kernels: 445 us -> 370 us  [the longest x2 316 us: layer_step(): pl.pallas_call(functools.partial(layer_kernel, maps, size, chunk, n_out,...]
    dot_general x0 -> x4, matrix products: none -> 64.9 us  [the longest x3 44.9 us: own_back(): lax.dot_general(one, other, TN, preferred_element_type=F32)]
    all_gather x4 -> x5, waiting for transfers between devices: 51.2 us -> 0.06 us  [gather(): return lax.all_gather(one, 'dp', tiled=True)]
    dot_general x3, matrix products: 52.1 us -> 43.2 us  [matmul_t(): return lax.dot_general(a, w, NT, preferred_element_type=F32).astype(BF16)]
    dynamic_slice x0 -> x4, local copies, waits for them, and re-layouts: none -> 7.36 us  [step(): lax.dynamic_slice(one, (0, 0, start), (1, one.shape[1], each))[0]]
  transfers between devices with their start and end apart: 4 -> 5, of which waited for: 1 -> 0; matrix products, arithmetic and copies ran while one was open for 18% -> 32% of each run, Pallas kernels for 36% -> 56%
where the time goes in v2:
time: 574 us; the launch traced here: 565 us
  Pallas kernels  370 us (64%)
  matrix products  159 us (28%)
  between operations  14.2 us (2%)
  other arithmetic  11.2 us (2%)
  local copies, waits for them, and re-layouts  9.37 us (2%)
    pallas_call x2, Pallas kernels, layer_step(): pl.pallas_call(functools.partial(layer_kernel, maps, size, chunk, n_out,...  316 us
    dot_general x3, matrix products, own_back(): lax.dot_general(one, other, TN, preferred_element_type=F32)  44.9 us
    dot_general x3, matrix products, matmul_t(): return lax.dot_general(a, w, NT, preferred_element_type=F32).astype(BF16)  43.2 us
    pallas_call x1, Pallas kernels, update_step(): pl.pallas_call(functools.partial(update_kernel, len(done)), grid=(blocks,...  28.7 us
    pallas_call x1, Pallas kernels, part_grads(): pl.pallas_call(functools.partial(part_kernel, chunk, n_out), in_specs=[pl...  25.1 us
    dot_general x1, matrix products, matmul(): return jnp.dot(a, w, preferred_element_type=F32).astype(BF16)  24.2 us
    dot_general x1, matrix products, own_back(): jnp.dot(a, up, preferred_element_type=F32)  20 us
    dot_general x1, matrix products, own_chain(): jnp.dot(a0, gate0, preferred_element_type=F32)  13.6 us
  transfers between devices with their start and end apart: 5, of which 0 were waited for; matrix products, arithmetic and copies ran while one was open for 32% of the time, Pallas kernels for 56%

profile of v2, /device:TPU:112, one launch (start us, length us, event | category | flops | bytes accessed | tf_op | source)
XLA Modules:
  0.0 564.8 jit_solution(7052689584784123272)
XLA Ops:
  7.2 0.1 all-gather.15.cloned.1.call-start
  7.3 0.7 all-gather.15.cloned.1.call-update
  8.0 0.1 all-gather.9.cloned.1.call-start
  8.1 2.1 fusion.30
  10.1 13.6 %fusion.18 = f32[1024,3200]{1,0:T(8,128)} fusion(bf16[2,1024,3200]{2,1,0:T(8,128)(2,1)} %refs_6_.5, bf16[1,1024,1024]{2,1,0:T(8,128)(2,1)} %param.11, f32[1024]{0:T(1024)S(1)} %add_rsqrt_fusion.1), kind=kOutput, calls=%fused_computation.27 | convolution fusion | flops 6714032128 | bytes 21762048 | tf_op jit(solution)/shard_map/dot_general | solution.py:225
  23.8 24.2 %fusion.34 = (f32[1024]{0:T(1024)S(1)}, bf16[1024,1024]{1,0:T(8,128)(2,1)S(1)}) fusion(bf16[2,3200,1024]{2,1,0:T(8,128)(2,1)} %refs_8_.5, f32[1024,3200]{1,0:T(8,128)} %fusion.18, bf16[2,1024,3200]{2,1,0:T(8,128)(2,1)} %refs_7_.5, bf16[1,1024,1024]{2,1,0:T(8,128)(2,1)} %param.11, f32[1024]{0:T(1024)S(1)} %add_rsqrt_fusion.1), kind=kOutput, calls=%fused_computation.45 | convolution fusion | flops 13452966912 | bytes 32514048 | tf_op jit(solution)/shard_map/dot_general | solution.py:210
  48.0 1.7 fusion.35
  49.7 0.1 all-gather.9.cloned.1.call-update
  49.8 0.1 all-gather.7.cloned.1.call-start
  49.9 3.3 fusion.31
  53.2 0.1 all-gather.7.cloned.1.call-update
  53.2 0.2 all-gather.11.cloned.1.call-start
  53.5 0.0 copy-start.1
  53.5 12.6 %convolution_convert_fusion = bf16[1024,3200]{1,0:T(8,128)(2,1)} fusion(bf16[2,3200,1024]{2,1,0:T(8,128)(2,1)} %refs_8_.5, bf16[1,1024,1024]{2,1,0:T(8,128)(2,1)} %param.12), kind=kOutput, calls=%fused_computation.9 | convolution fusion | flops 6714163200 | bytes 15204352 | tf_op jit(solution)/shard_map/dot_general | solution.py:214
  66.1 0.0 copy-done.1
  66.1 13.1 %fusion.7 = f32[1024,3200]{1,0:T(8,128)} fusion(bf16[1024,1024]{1,0:T(8,128)(2,1)S(1)} %copy-done.1, bf16[2,1024,3200]{2,1,0:T(8,128)(2,1)} %refs_6_.5), kind=kOutput, calls=%fused_computation.17 | convolution fusion | flops 6710886400 | bytes 21757952 | tf_op jit(solution)/shard_map/dot_general | solution.py:234
  79.2 20.0 %fusion.1 = (bf16[1024,3200]{1,0:T(8,128)(2,1)}, f32[1024,3200]{1,0:T(8,128)}) fusion(bf16[1024,3200]{1,0:T(8,128)(2,1)} %convolution_convert_fusion, f32[1024,3200]{1,0:T(8,128)} %fusion.7, bf16[1024,1024]{1,0:T(8,128)(2,1)} %fusion.35, bf16[2,1024,3200]{2,1,0:T(8,128)(2,1)} %refs_7_.5), kind=kOutput, calls=%fused_computation.3 | convolution fusion | flops 6746931200 | bytes 47972352 | tf_op jit(solution)/shard_map/dot_general | solution.py:234
  99.2 13.3 %fusion.5 = bf16[1024,1024]{1,0:T(8,128)(2,1)} fusion(bf16[1024,3200]{1,0:T(8,128)(2,1)} %get-tuple-element.71, bf16[2,1024,3200]{2,1,0:T(8,128)(2,1)} %refs_6_.5), kind=kOutput, calls=%fused_computation.15 | convolution fusion | flops 6710886400 | bytes 15204352 | tf_op jit(solution)/shard_map/dot_general | solution.py:214
  112.5 17.2 %fusion.37 = (f32[1024]{0:T(1024)S(1)}, bf16[1024,1024]{1,0:T(8,128)(2,1)}) fusion(bf16[1024,1024]{1,0:T(8,128)(2,1)S(1)} %get-tuple-element.70, bf16[1024,1024]{1,0:T(8,128)(2,1)} %fusion.5, bf16[2,1024,3200]{2,1,0:T(8,128)(2,1)} %refs_7_.5, bf16[1024,3200]{1,0:T(8,128)(2,1)} %convolution_convert_fusion, f32[1024,3200]{1,0:T(8,128)} %fusion.7), kind=kOutput, calls=%fused_computation.48 | convolution fusion | flops 6740114432 | bytes 32509952 | tf_op jit(solution)/shard_map/dot_general | solution.py:214
  129.8 4.0 fusion.39
  133.8 0.1 all-gather.11.cloned.1.call-update
  133.8 0.1 all-gather.13.cloned.1.call-start
  133.9 2.0 dynamic-slice_bitcast_fusion.wd
  135.9 2.5 constant_dynamic-slice_fusion.1
  138.4 1.6 constant_dynamic-slice_fusion
  139.9 0.0 copy-start
  139.9 15.9 %fusion.53.refs_12_ = f32[1024,3200]{1,0:T(8,128)} fusion(bf16[1024,1024]{1,0:T(8,128)(2,1)} %fusion.35, bf16[1024,3200]{1,0:T(8,128)(2,1)} %convolution_convert_fusion, f32[1024,3200]{1,0:T(8,128)} %fusion.7), kind=kOutput, calls=%fused_computation.64 | convolution fusion | flops 6733824000 | bytes 34865152 | tf_op jit(solution)/shard_map/dot_general | solution.py:242
  155.9 2.2 copy.41
  158.1 1.1 copy.42
  159.2 0.0 copy-done
  159.2 0.0 copy-start.2
  159.2 15.6 %fusion.4.refs_13_ = f32[3200,1024]{1,0:T(8,128)} fusion(f32[1024,3200]{1,0:T(8,128)} %get-tuple-element.72, bf16[1,1024,1024]{2,1,0:T(8,128)(2,1)S(1)} %copy-done, f32[1024,3200]{1,0:T(8,128)} %fusion.7), kind=kOutput, calls=%fused_computation.14 | convolution fusion | flops 6730547200 | bytes 41418752 | tf_op jit(solution)/shard_map/dot_general | solution.py:242
  174.8 0.0 copy-done.2
  174.8 13.4 %fusion.62.refs_11_ = f32[1024,3200]{1,0:T(8,128)} fusion(bf16[1024,1024]{1,0:T(8,128)(2,1)S(1)} %copy-done.2, bf16[1024,3200]{1,0:T(8,128)(2,1)} %get-tuple-element.71), kind=kOutput, calls=%fused_computation.65 | convolution fusion | flops 6710886400 | bytes 21757952 | tf_op jit(solution)/shard_map/dot_general | solution.py:242
  188.2 0.0 all-gather.15.cloned.1.call-done
  188.2 0.0 all-gather.9.cloned.1.call-done.refs_0_
  188.2 181.6 %shard_map.178 = (bf16[2,1024,3200]{2,1,0:T(8,128)(2,1)}, bf16[2,1024,3200]{2,1,0:T(8,128)(2,1)}, bf16[2,3200,1024]{2,1,0:T(8,128)(2,1)}, f32[2,1024,3200]{2,1,0...) custom-call(bf16[4096,1024]{1,0:T(8,128)(2,1)} %all-gather.9.cloned., ...), custom_call_target="tpu_custom_call" | custom-call | flops 120795955200 | bytes 196608000 | tf_op jit(solution)/shard_map/pallas_call | solution.py:105
  369.8 0.0 all-gather.7.cloned.1.call-done.a_all.refs_0_
  369.8 0.0 all-gather.11.cloned.1.call-done.dh_all.refs_1_
  369.8 25.1 %part_grads.1.refs_20_ = bf16[960,1024]{1,0:T(8,128)(2,1)} custom-call(bf16[4096,1024]{1,0:T(8,128)(2,1)} %all-gather.7.cloned.1.call-done.a_all.refs_0_, bf16[4096,1024]{1,0:T(8,128)(2,1)} %all-gather.11.cloned.1.call-done.dh_all.refs_1_, bf16[320,1024]{1,0:T(8,128)(2,1)} %bitcast.69, bf16[320,1024]{1,0:T(8,128)(2,1)} %bitcast.70, ...), custom_call_target="tpu_custom_call" | custom-call | flops 16106127360 | bytes 16777216 | tf_op jit(solution)/shard_map/part_grads/pallas_call | solution.py:172
  394.9 0.1 all-gather.13.cloned.1.call-update
  395.0 134.3 %shard_map.179 = (bf16[2,1024,3200]{2,1,0:T(8,128)(2,1)}, bf16[2,1024,3200]{2,1,0:T(8,128)(2,1)}, bf16[2,3200,1024]{2,1,0:T(8,128)(2,1)}, f32[2,1024,3200]{2,1,0...) custom-call(bf16[4096,1024]{1,0:T(8,128)(2,1)} %all-gather.7.cloned., ...), custom_call_target="tpu_custom_call", output_to_operand_aliasing={{0}: (11, {}), {1}: (12, {}), {2}: (13, {}), {3}: (14, {}),... | custom-call | flops 96636764160 | bytes 117964800 | tf_op jit(solution)/shard_map/pallas_call | solution.py:105
  529.3 0.0 all-gather.13.cloned.1.call-done.refs_0_.refs_1_.refs_2_.refs_3_.refs_4_.refs_5_
  529.3 28.7 %shard_map.180 = (bf16[2,1024,3200]{2,1,0:T(8,128)(2,1)}, bf16[2,1024,3200]{2,1,0:T(8,128)(2,1)}, bf16[2,3200,1024]{2,1,0:T(8,128)(2,1)}, f32[2,1024,3200]{2,1,0...) custom-call(bf16[3840,1024]{1,0:T(8,128)(2,1)} %all-gather.13.cloned, ...), custom_call_target="tpu_custom_call", output_to_operand_aliasing={{0}: (15, {}), {1}: (16, {}), {2}: (17, {}), {3}: (18, {}),... | custom-call | flops 78643200 | bytes 86507520 | tf_op jit(solution)/shard_map/pallas_call | solution.py:197
  (3 shorter events, 0.0 us)
Async XLA Ops:
  7.2 181.0 %all-gather.15.cloned.1.call-start = ((), (), s32[]{:S(2)}) async-start(), calls=%async_computation.4 | async-start | bytes 10485760 | tf_op jit(solution)/shard_map/all_gather | solution.py:258
  8.0 180.2 %all-gather.9.cloned.1.call-start = ((), (), s32[]{:S(2)}) async-start(), calls=%async_computation.1 | async-start | bytes 10485760 | tf_op jit(solution)/shard_map/all_gather | solution.py:258
  49.8 320.0 %all-gather.7.cloned.1.call-start = ((), (), s32[]{:S(2)}) async-start(), calls=%async_computation | async-start | bytes 10485760 | tf_op jit(solution)/shard_map/all_gather | solution.py:258
  53.2 316.6 %all-gather.11.cloned.1.call-start = ((), (), s32[]{:S(2)}) async-start(), calls=%async_computation.2 | async-start | bytes 10485760 | tf_op jit(solution)/shard_map/all_gather | solution.py:258
  53.5 12.6 %copy-start.1 = (bf16[1024,1024]{1,0:T(8,128)(2,1)S(1)}, bf16[1024,1024]{1,0:T(8,128)(2,1)}, u32[]{:S(2)}) copy-start(bf16[1024,1024]{1,0:T(8,128)(2,1)} %fusion.35) | copy-start | bytes 6291460
  133.8 395.5 %all-gather.13.cloned.1.call-start = ((), (), s32[]{:S(2)}) async-start(), calls=%async_computation.3 | async-start | bytes 9830400 | tf_op jit(solution)/shard_map/all_gather | solution.py:258
  139.9 19.3 %copy-start = (bf16[1,1024,1024]{2,1,0:T(8,128)(2,1)S(1)}, bf16[1,1024,1024]{2,1,0:T(8,128)(2,1)}, u32[]{:S(2)}) copy-start(bf16[1,1024,1024]{2,1,0:T(8,128)(2,1)} %param.12) | copy-start | bytes 6291460
  159.2 15.6 %copy-start.2 = (bf16[1024,1024]{1,0:T(8,128)(2,1)S(1)}, bf16[1024,1024]{1,0:T(8,128)(2,1)}, u32[]{:S(2)}) copy-start(bf16[1024,1024]{1,0:T(8,128)(2,1)} %fusion.35) | copy-start | bytes 6291460
Sparse Core Ops, SparseCore 0:
  9.6 81.8 all-gather.14
  93.6 79.9 all-gather.8
  175.1 79.9 all-gather.6
  256.5 79.9 all-gather.10
  395.1 78.4 all-gather.12

commit v3 on v2

--- a/solution.py
+++ b/solution.py
@@ -10,7 +10,6 @@
 
 F32, BF16 = jnp.float32, jnp.bfloat16
 NT = (((1,), (1,)), ((), ()))
-TN = (((0,), (0,)), ((), ()))
 
 
 def adam_store(g, w, m_ref, v_ref, w_out, m_out, v_out):
@@ -23,10 +22,10 @@
 
 
 def layer_kernel(pieces, tokens, chunk, n_out, bases, extra, *refs):
-    a_all, dh_all, wg, wu, wd, mg, mu, md, vg, vu, vd = refs[:11]
-    base = refs[11 : 11 + bases]
-    rest = refs[11 + bases + extra :]
-    wgo, wuo, wdo, mgo, muo, mdo, vgo, vuo, vdo, a, dh, wgt, wut, hid, dgt, dut, sem = rest
+    a_all, dh_all, wgt, wut, wg, wu, wd, mg, mu, md, vg, vu, vd = refs[:13]
+    base = refs[13 : 13 + bases]
+    rest = refs[13 + bases + extra :]
+    wgo, wuo, wdo, mgo, muo, mdo, vgo, vuo, vdo, a, dh, hid, dgt, dut, sem = rest
     f, s = pl.program_id(0), pl.program_id(1)
     size = tokens
     a_at, dh_at = pieces
@@ -49,9 +48,6 @@
 
     @pl.when(s == 0)
     def _():
-        wgt[...] = wg[0].T
-        wut[...] = wu[0].T
-
         def one(i, _):
             @pl.when((f == 0) & (lax.rem(i, size // chunk) == 0))
             def _():
@@ -77,14 +73,14 @@
         cols = pl.ds(pl.multiple_of((s - 1) * n_out, n_out), n_out)
         ac, dc = a[:, cols], dh[:, cols]
         g = jnp.dot(dgt[...], ac, preferred_element_type=F32).T
-        adam_store(g + base[0][...] if bases else g, wg[0, cols, :], mg, vg, wgo, mgo, vgo)
+        adam_store(g + base[0][...] if bases else g, wg[0], mg, vg, wgo, mgo, vgo)
         g = jnp.dot(dut[...], ac, preferred_element_type=F32).T
-        adam_store(g + base[1][...] if bases else g, wu[0, cols, :], mu, vu, wuo, muo, vuo)
+        adam_store(g + base[1][...] if bases else g, wu[0], mu, vu, wuo, muo, vuo)
         g = jnp.dot(hid[...], dc, preferred_element_type=F32)
         adam_store(g + base[2][...] if bases else g, wd[0, :, cols], md, vd, wdo, mdo, vdo)
 
 
-def layer_step(number, a, dh, pieces, w, m, v, done=None, base=None, skip=0, after=(), ffb=640, chunk=256, n_out=256):
+def layer_step(number, a, dh, pieces, turned, w, m, v, done=None, base=None, skip=0, after=(), ffb=640, chunk=1024, n_out=256):
     count, size, *maps = pieces
     d = a.shape[1]
     rows = count * size
@@ -92,30 +88,33 @@
     chunks = d // n_out
     late = lambda s: jnp.maximum(s - 1, 0)
     apart = pl.BlockSpec(memory_space=pl.ANY)
-    w_in = [pl.BlockSpec((1, d, ffb), lambda f, s: (number, 0, f + skip))] * 2 + [
-        pl.BlockSpec((1, ffb, d), lambda f, s: (number, f + skip, 0))
-    ]
     tile = [pl.BlockSpec((1, n_out, ffb), lambda f, s: (number, late(s), f + skip))] * 2 + [
         pl.BlockSpec((1, ffb, n_out), lambda f, s: (number, f + skip, late(s)))
     ]
-    flat = [pl.BlockSpec((n_out, ffb), lambda f, s: (late(s), f))] * 2 + [pl.BlockSpec((ffb, n_out), lambda f, s: (f, late(s)))]
+    flat = [pl.BlockSpec((n_out, ffb), lambda f, s: (late(s), f + skip))] * 2 + [
+        pl.BlockSpec((ffb, n_out), lambda f, s: (f + skip, late(s)))
+    ]
     out_shape = [jax.ShapeDtypeStruct(x.shape, x.dtype) for x in (*w, *m, *v)]
     base, extra, after = list(base or []), list(done or []), list(after)
-    first = 11 + len(base)
+    first = 13 + len(base)
     return pl.pallas_call(
         functools.partial(layer_kernel, maps, size, chunk, n_out, len(base), len(extra) + len(after)),
         grid=(ff // ffb, chunks + 1),
-        in_specs=[apart] * 2 + w_in + tile + tile + flat[: len(base)] + [apart] * (len(extra) + len(after)),
+        in_specs=[apart] * 2
+        + [pl.BlockSpec((ffb, d), lambda f, s: (f + skip, 0))] * 2
+        + tile[:2]
+        + [pl.BlockSpec((1, ffb, d), lambda f, s: (number, f + skip, 0))]
+        + tile * 2
+        + flat[: len(base)] + [apart] * (len(extra) + len(after)),
         out_specs=tile * 3,
         out_shape=out_shape,
         scratch_shapes=[pltpu.VMEM((rows, d), BF16)] * 2
-        + [pltpu.VMEM((ffb, d), BF16)] * 2
         + [pltpu.VMEM((ffb, rows), BF16)] * 3
         + [pltpu.SemaphoreType.DMA((2, count))],
         input_output_aliases={first + i: i for i in range(len(extra))},
         compiler_params=pltpu.CompilerParams(vmem_limit_bytes=67_043_328, dimension_semantics=("arbitrary", "arbitrary")),
         cost_estimate=pl.CostEstimate(flops=12 * rows * d * ff, bytes_accessed=20 * 3 * d * ff, transcendentals=0),
-    )(a, dh, *w, *m, *v, *base, *extra, *after)
+    )(a, dh, *turned, *w, *m, *v, *base, *extra, *after)
 
 
 def part_kernel(chunk, n_out, a_all, dh_all, wgt, wut, wd, out, a, dh, hid, dgt, dut, sem):
@@ -165,7 +164,7 @@
     lax.fori_loop(0, a.shape[1] // n_out, two, 0)
 
 
-def part_grads(a, dh, wgt, wut, wd, pieces, chunk=512, n_out=256):
+def part_grads(a, dh, wgt, wut, wd, pieces, chunk=512, n_out=1024):
     rows, d = a.shape
     each = wgt.shape[0]
     inside = pl.BlockSpec(memory_space=pltpu.VMEM)
@@ -206,12 +205,78 @@
     )(*[grads] * 6, *w, *m, *v, *done)
 
 
+def own_kernel(chunk, n_out, a, dh, wg, wu, wd, pg, pu, pd, *rest):
+    wgt, wut, *da, hid, dgt, dut = rest
+    wgt[...] = wg[0].T
+    wut[...] = wu[0].T
+
+    if da:
+
+        @pl.when(pl.program_id(0) == 0)
+        def _():
+            da[0][...] = jnp.zeros_like(da[0])
+
+    def one(i, _):
+        rows = pl.ds(pl.multiple_of(i * chunk, chunk), chunk)
+        ac, dc = a[rows, :], dh[rows, :]
+        g = lax.dot_general(wgt[...], ac, NT, preferred_element_type=F32)
+        u = lax.dot_general(wut[...], ac, NT, preferred_element_type=F32)
+        d = lax.dot_general(wd[0], dc, NT, preferred_element_type=F32).astype(BF16).astype(F32)
+        sig = 1.0 / (1.0 + jnp.exp(-g))
+        silu = g * sig
+        hid[:, rows] = (silu * u).astype(BF16)
+        du, dg = (d * silu).astype(BF16), (d * u * (sig + silu * (1.0 - sig))).astype(BF16)
+        dut[:, rows] = du
+        dgt[:, rows] = dg
+        return 0
+
+    lax.fori_loop(0, a.shape[0] // chunk, one, 0)
+
+    def two(i, _):
+        cols = pl.ds(pl.multiple_of(i * n_out, n_out), n_out)
+        ac, dc = a[:, cols], dh[:, cols]
+        pg[cols, :] = jnp.dot(dgt[...], ac, preferred_element_type=F32).T
+        pu[cols, :] = jnp.dot(dut[...], ac, preferred_element_type=F32).T
+        pd[:, cols] = jnp.dot(hid[...], dc, preferred_element_type=F32)
+        return 0
+
+    def three(i, _):
+        cols = pl.ds(pl.multiple_of(i * n_out, n_out), n_out)
+        da[0][:, cols] += jnp.dot(wg[0], dgt[:, cols], preferred_element_type=F32) + jnp.dot(wu[0], dut[:, cols], preferred_element_type=F32)
+        return 0
+
+    if da:
+        lax.fori_loop(0, a.shape[0] // n_out, three, 0)
+
+    lax.fori_loop(0, a.shape[1] // n_out, two, 0)
+
+
+def own_grads(number, a, dh, w, want_da, skip=0, ffb=640, chunk=1024, n_out=1024):
+    rows, d = a.shape
+    ff = w[0].shape[2]
+    whole = pl.BlockSpec((rows, d), lambda f: (0, 0), pipeline_mode=pl.Buffered(1))
+    w_in = [pl.BlockSpec((1, d, ffb), lambda f: (number, 0, f + skip))] * 2 + [pl.BlockSpec((1, ffb, d), lambda f: (number, f + skip, 0))]
+    out = [pl.BlockSpec((d, ffb), lambda f: (0, f + skip))] * 2 + [pl.BlockSpec((ffb, d), lambda f: (f + skip, 0))]
+    out_shape = [jax.ShapeDtypeStruct(one.shape[1:], F32) for one in w]
+    out += [pl.BlockSpec((ffb, d), lambda f: (f + skip, 0))] * 2
+    out_shape += [jax.ShapeDtypeStruct((ff, d), BF16)] * 2
+    if want_da:
+        out, out_shape = out + [pl.BlockSpec((d, rows), lambda f: (0, 0))], out_shape + [jax.ShapeDtypeStruct((d, rows), F32)]
+    blocks = ff // ffb - skip
+    return pl.pallas_call(
+        functools.partial(own_kernel, chunk, n_out),
+        grid=(blocks,),
+        in_specs=[whole, whole] + w_in,
+        out_specs=out,
+        out_shape=out_shape,
+        scratch_shapes=[pltpu.VMEM((ffb, rows), BF16)] * 3,
+        compiler_params=pltpu.CompilerParams(vmem_limit_bytes=67_043_328, dimension_semantics=("arbitrary",)),
+        cost_estimate=pl.CostEstimate(flops=(16 if want_da else 12) * rows * d * ffb * blocks, bytes_accessed=18 * d * ffb * blocks, transcendentals=0),
+    )(a, dh, *w)
+
+
 def matmul(a, w):
     return jnp.dot(a, w, preferred_element_type=F32).astype(BF16)
-
-
-def matmul_t(a, w):
-    return lax.dot_general(a, w, NT, preferred_element_type=F32).astype(BF16)
 
 
 def scale_of(h):
@@ -220,7 +285,7 @@
 
 
 def own_chain(x, w):
-    (gate0, gate1), (up0, up1), (down0, down1) = w
+    gate0, up0, down0 = w
     a0 = (x.astype(F32) * scale_of(x)).astype(BF16)
     g, u = jnp.dot(a0, gate0, preferred_element_type=F32), jnp.dot(a0, up0, preferred_element_type=F32)
     h = x + matmul((jax.nn.silu(g) * u).astype(BF16), down0)
@@ -230,17 +295,10 @@
     return a0, h, a1, scale
 
 
-def own_back(h, a, scale, dy, gate, up, down):
-    g, u = jnp.dot(a, gate, preferred_element_type=F32), jnp.dot(a, up, preferred_element_type=F32)
-    d = matmul_t(dy, down).astype(F32)
-    sig = jax.nn.sigmoid(g)
-    silu = g * sig
-    dg, du, hidden = (d * u * (sig + silu * (1.0 - sig))).astype(BF16), (d * silu).astype(BF16), (silu * u).astype(BF16)
-    da = matmul_t(dg, gate) + matmul_t(du, up)
-    wide, da = h.astype(F32), da.astype(F32)
+def own_back(h, scale, da, dy):
+    wide, da = h.astype(F32), da.astype(BF16).astype(F32)
     back = da * scale - wide * (scale * scale * scale) * jnp.mean(da * wide, -1, keepdims=True)
-    parts = [lax.dot_general(one, other, TN, preferred_element_type=F32) for one, other in ((a, dg), (a, du), (hidden, dy))]
-    return dy + back.astype(BF16), parts
+    return dy + back.astype(BF16)
 
 
 BLOCK, SHARED = 640, 2
@@ -257,11 +315,12 @@
         def gather(one):
             return lax.all_gather(one, "dp", tiled=True)
 
-        pairs = tuple((one[0], one[1]) for one in w)
-        a0, h1, a1, scale = own_chain(x, pairs)
+        a0, h1, a1, scale = own_chain(x, tuple(one[0] for one in w))
         dy_all = gather(dy)
         a1_all = gather(a1)
-        dh1, parts = own_back(h1, a1, scale, dy, *(one[1] for one in w))
+        *parts1, gate1, up1, da = own_grads(1, a1, dy, w, True)
+        dh1 = own_back(h1, scale, da.T, dy)
+        *parts0, gate0, up0 = own_grads(0, a0, dh1, w, False, skip=SHARED)
         a0, _ = lax.optimization_barrier((a0, a1))
         a0_all, dh1_all = gather(a0), gather(dh1)
         others = lambda i: lax.rem(lax.axis_index("dp") + 1 + i, n)
@@ -269,12 +328,11 @@
         start = lax.axis_index("dp") * each
         gate, up = (lax.dynamic_slice(one, (0, 0, start), (1, one.shape[1], each))[0].T for one in w[:2])
         down = lax.dynamic_slice(w[2], (0, start, 0), (1, each, w[2].shape[2]))[0]
-        new = layer_step(1, a1_all, dy_all, (n - 1, x.shape[0], others, others), w, m, v, base=parts)
+        new = layer_step(1, a1_all, dy_all, (n - 1, x.shape[0], others, others), (gate1, up1), w, m, v, base=parts1, after=parts0[:1])
         a0_all, *new = lax.optimization_barrier((a0_all, *new))
         mine = part_grads(a0_all, dh1_all, gate, up, down, n)
         grads = gather(mine)
-        whole = (n, x.shape[0], lambda i: i, lambda i: i)
-        new = layer_step(0, a0_all, dh1_all, whole, w, m, v, done=new, skip=SHARED, after=(mine,))
+        new = layer_step(0, a0_all, dh1_all, (n - 1, x.shape[0], others, others), (gate0, up0), w, m, v, base=parts0, done=new, skip=SHARED, after=(mine,))
         return tuple(update_step(0, grads, w, m, v, new, SHARED))
 
     return jax.shard_map(

time: 574 us -> 534 us (0.930)
  matrix products: 159 us -> 37.9 us
  Pallas kernels: 370 us -> 446 us
    dot_general x8 -> x0, matrix products: 121 us -> none  [the longest x3 44.9 us: own_back(): lax.dot_general(one, other, TN, preferred_element_type=F32)]
    pallas_call x0 -> x2, Pallas kernels: none -> 103 us  [own_grads(): pl.pallas_call(functools.partial(own_kernel, chunk, n_out), grid=(blocks,...]
    pallas_call x2, Pallas kernels: 316 us -> 290 us  [layer_step(): pl.pallas_call(functools.partial(layer_kernel, maps, size, chunk, n_out,...]
  transfers between devices with their start and end apart: 5 -> 5, of which waited for: 0 -> 0; matrix products, arithmetic and copies ran while one was open for 32% -> 12% of each run, Pallas kernels for 56% -> 75%
where the time goes in v3:
time: 534 us; the launch traced here: 526 us
  Pallas kernels  446 us (84%)
  matrix products  37.9 us (7%)
  between operations  14.4 us (3%)
  other arithmetic  14.1 us (3%)
  local copies, waits for them, and re-layouts  11.5 us (2%)
    pallas_call x2, Pallas kernels, layer_step(): pl.pallas_call(functools.partial(layer_kernel, maps, size, chunk, n_out,...  290 us
    pallas_call x2, Pallas kernels, own_grads(): pl.pallas_call(functools.partial(own_kernel, chunk, n_out), grid=(blocks,...  103 us
    pallas_call x1, Pallas kernels, update_step(): pl.pallas_call(functools.partial(update_kernel, len(done)), grid=(blocks,...  28.7 us
    pallas_call x1, Pallas kernels, part_grads(): pl.pallas_call(functools.partial(part_kernel, chunk, n_out), in_specs=[pl...  24.6 us
    dot_general x1, matrix products, matmul(): return jnp.dot(a, w, preferred_element_type=F32).astype(BF16)  24.3 us
    dot_general x1, matrix products, own_chain(): jnp.dot(a0, gate0, preferred_element_type=F32)  13.6 us
  transfers between devices with their start and end apart: 5, of which 0 were waited for; matrix products, arithmetic and copies ran while one was open for 12% of the time, Pallas kernels for 75%

profile of v3, /device:TPU:112, one launch (start us, length us, event | category | flops | bytes accessed | tf_op | source)
XLA Modules:
  0.0 525.6 jit_solution(983063603204287960)
XLA Ops:
  7.2 0.1 all-gather.15.cloned.1.call-start
  7.3 0.7 all-gather.15.cloned.1.call-update
  8.0 0.1 all-gather.9.cloned.1.call-start
  8.1 2.1 fusion.11
  10.1 13.6 %fusion.4 = f32[1024,3200]{1,0:T(8,128)} fusion(bf16[2,1024,3200]{2,1,0:T(8,128)(2,1)} %refs_6_.5, bf16[1,1024,1024]{2,1,0:T(8,128)(2,1)} %param.11, f32[1024]{0:T(1024)S(1)} %add_rsqrt_fusion.1), kind=kOutput, calls=%fused_computation.8 | convolution fusion | flops 6714032128 | bytes 21762048 | tf_op jit(solution)/shard_map/dot_general | solution.py:290
  23.8 24.3 %fusion.13 = (f32[1024]{0:T(1024)S(1)}, bf16[1024,1024]{1,0:T(8,128)(2,1)S(1)}) fusion(bf16[2,3200,1024]{2,1,0:T(8,128)(2,1)} %refs_8_.5, f32[1024,3200]{1,0:T(8,128)} %fusion.4, bf16[2,1024,3200]{2,1,0:T(8,128)(2,1)} %refs_7_.5, bf16[1,1024,1024]{2,1,0:T(8,128)(2,1)} %param.11, f32[1024]{0:T(1024)S(1)} %add_rsqrt_fusion.1), kind=kOutput, calls=%fused_computation.18 | convolution fusion | flops 13452966912 | bytes 32514048 | tf_op jit(solution)/shard_map/dot_general | solution.py:279
  48.0 0.0 copy-start
  48.1 0.7 multiply_multiply_fusion
  48.7 0.0 copy-start.1
  48.7 0.7 copy-done
  49.4 0.0 copy-done.1
  49.4 1.7 fusion.14.a
  51.1 0.1 all-gather.9.cloned.1.call-update
  51.2 0.1 all-gather.7.cloned.1.call-start
  51.2 3.3 fusion.12.a
  54.6 0.1 all-gather.7.cloned.1.call-update
  54.6 0.3 all-gather.11.cloned.1.call-start
  54.9 70.5 %shard_map.178 = (f32[1024,3200]{1,0:T(8,128)}, f32[1024,3200]{1,0:T(8,128)}, f32[3200,1024]{1,0:T(8,128)}, bf16[3200,1024]{1,0:T(8,128)(2,1)}, bf16[3200,1024]{1,0:T(8,128)(2,1)}, /*index=5*/f32[1024,1024]{1,0:T(8,128)}) custom-call(bf16[1024,1024]{1,0:T(8,128)(2,1)} %fusion.14.a, bf16[1024,1024]{1,0:T(8,128)(2,1)} %bitcast.47, ...), custom_call_target="tpu_custom_call" | custom-call | flops 53687091200 | bytes 58982400 | tf_op jit(solution)/shard_map/pallas_call | solution.py:266
  125.5 0.0 copy-start.2
  125.5 0.0 copy-start.3
  125.5 3.4 copy.39
  128.9 2.2 fusion.18
  131.1 0.0 copy-done.2
  131.2 0.0 copy-done.3
  131.2 4.1 fusion.20.dh
  135.2 0.1 all-gather.11.cloned.1.call-update
  135.3 0.5 all-gather.13.cloned.1.call-start
  135.8 2.0 dynamic-slice_bitcast_fusion.wd
  137.8 1.6 constant_dynamic-slice_fusion.1
  139.3 1.6 constant_dynamic-slice_fusion
  140.9 1.2 copy.40
  142.1 1.1 copy.41
  143.2 32.1 %shard_map.179 = (f32[1024,3200]{1,0:T(8,128)}, f32[1024,3200]{1,0:T(8,128)}, f32[3200,1024]{1,0:T(8,128)}, bf16[3200,1024]{1,0:T(8,128)(2,1)}, bf16[3200,1024]{1,0:T(8,128)(2,1)}) custom-call(bf16[1024,1024]{1,0:T(8,128)(2,1)} %fusion.12.a, bf16[1024,1024]{1,0:T(8,128)(2,1)} %fusion.20.dh, bf16[2,1024,3200]{2,1,0:T(8,128)(2,1)} %refs_6_.5, ...), custom_call_target="tpu_custom_call" | custom-call | flops 24159191040 | bytes 35389440 | tf_op jit(solution)/shard_map/pallas_call | solution.py:266
  175.3 0.0 all-gather.15.cloned.1.call-done
  175.3 0.0 all-gather.9.cloned.1.call-done.refs_0_
  175.3 179.8 %shard_map.180 = (bf16[2,1024,3200]{2,1,0:T(8,128)(2,1)}, bf16[2,1024,3200]{2,1,0:T(8,128)(2,1)}, bf16[2,3200,1024]{2,1,0:T(8,128)(2,1)}, f32[2,1024,3200]{2,1,0...) custom-call(bf16[4096,1024]{1,0:T(8,128)(2,1)} %all-gather.9.cloned., ...), custom_call_target="tpu_custom_call" | custom-call | flops 120795955200 | bytes 196608000 | tf_op jit(solution)/shard_map/pallas_call | solution.py:100
  355.1 0.0 all-gather.7.cloned.1.call-done.a_all.refs_0_
  355.1 0.0 all-gather.11.cloned.1.call-done.dh_all.refs_1_
  355.1 24.6 %part_grads.1.refs_25_ = bf16[960,1024]{1,0:T(8,128)(2,1)} custom-call(bf16[4096,1024]{1,0:T(8,128)(2,1)} %all-gather.7.cloned.1.call-done.a_all.refs_0_, bf16[4096,1024]{1,0:T(8,128)(2,1)} %all-gather.11.cloned.1.call-done.dh_all.refs_1_, bf16[320,1024]{1,0:T(8,128)(2,1)} %bitcast.48, bf16[320,1024]{1,0:T(8,128)(2,1)} %bitcast.49, ...), custom_call_target="tpu_custom_call" | custom-call | flops 16106127360 | bytes 16777216 | tf_op jit(solution)/shard_map/part_grads/pallas_call | solution.py:171
  379.7 0.1 all-gather.13.cloned.1.call-update
  379.8 110.1 %shard_map.181 = (bf16[2,1024,3200]{2,1,0:T(8,128)(2,1)}, bf16[2,1024,3200]{2,1,0:T(8,128)(2,1)}, bf16[2,3200,1024]{2,1,0:T(8,128)(2,1)}, f32[2,1024,3200]{2,1,0...) custom-call(bf16[4096,1024]{1,0:T(8,128)(2,1)} %all-gather.7.cloned., ...), custom_call_target="tpu_custom_call", output_to_operand_aliasing={{0}: (16, {}), {1}: (17, {}), {2}: (18, {}), {3}: (19, {}),... | custom-call | flops 72477573120 | bytes 117964800 | tf_op jit(solution)/shard_map/pallas_call | solution.py:100
  489.9 0.0 all-gather.13.cloned.1.call-done.refs_0_.refs_1_.refs_2_.refs_3_.refs_4_.refs_5_
  489.9 28.7 %shard_map.182 = (bf16[2,1024,3200]{2,1,0:T(8,128)(2,1)}, bf16[2,1024,3200]{2,1,0:T(8,128)(2,1)}, bf16[2,3200,1024]{2,1,0:T(8,128)(2,1)}, f32[2,1024,3200]{2,1,0...) custom-call(bf16[3840,1024]{1,0:T(8,128)(2,1)} %all-gather.13.cloned, ...), custom_call_target="tpu_custom_call", output_to_operand_aliasing={{0}: (15, {}), {1}: (16, {}), {2}: (17, {}), {3}: (18, {}),... | custom-call | flops 78643200 | bytes 86507520 | tf_op jit(solution)/shard_map/pallas_call | solution.py:196
  (2 shorter events, 0.0 us)
Async XLA Ops:
  7.2 168.1 %all-gather.15.cloned.1.call-start = ((), (), s32[]{:S(2)}) async-start(), calls=%async_computation.4 | async-start | bytes 10485760 | tf_op jit(solution)/shard_map/all_gather | solution.py:316
  8.0 167.3 %all-gather.9.cloned.1.call-start = ((), (), s32[]{:S(2)}) async-start(), calls=%async_computation.1 | async-start | bytes 10485760 | tf_op jit(solution)/shard_map/all_gather | solution.py:316
  48.0 1.3 copy-start
  48.7 0.7 copy-start.1
  51.2 303.9 %all-gather.7.cloned.1.call-start = ((), (), s32[]{:S(2)}) async-start(), calls=%async_computation | async-start | bytes 10485760 | tf_op jit(solution)/shard_map/all_gather | solution.py:316
  54.6 300.5 %all-gather.11.cloned.1.call-start = ((), (), s32[]{:S(2)}) async-start(), calls=%async_computation.2 | async-start | bytes 10485760 | tf_op jit(solution)/shard_map/all_gather | solution.py:316
  125.5 5.7 %copy-start.2 = (f32[1024]{0:T(1024)S(1)}, f32[1024]{0:T(1024)}, u32[]{:S(2)}) copy-start(f32[1024]{0:T(1024)} %copy-done.1) | copy-start | bytes 12292
  125.5 5.7 %copy-start.3 = (f32[1024]{0:T(1024)S(1)}, f32[1024]{0:T(1024)}, u32[]{:S(2)}) copy-start(f32[1024]{0:T(1024)} %get-tuple-element.89) | copy-start | bytes 12292
  135.3 354.7 %all-gather.13.cloned.1.call-start = ((), (), s32[]{:S(2)}) async-start(), calls=%async_computation.3 | async-start | bytes 9830400 | tf_op jit(solution)/shard_map/all_gather | solution.py:316
Sparse Core Ops, SparseCore 0:
  9.6 81.8 all-gather.14
  93.6 79.9 all-gather.8
  175.1 79.9 all-gather.6
  256.5 79.9 all-gather.10
  379.9 78.0 all-gather.12
